TPU v7x, 256 devices: a whole 4x4x8 slice. The times are simulated.
256 devices in a mesh: ep: 8 (over z), tp: 32 (over y, x, core).
Axes of the slice: x: 4, y: 4, z: 8, core: 2. Of those that a mesh axis runs over, the one named last changes fastest.
Arguments:
- tokens: bfloat16 [768, 3072], P('ep', 'tp'), may hold values from -6 to 6
- cotangent: bfloat16 [768, 3072], P('ep', 'tp'), may hold values from -6 to 6
- expert_ids: int32 [768, 2], P('ep'), may hold values from 0 to 7, all different within a row; in each aligned block of 96 rows (0 to 95, 96 to 191, ...) at most 40 rows name the same one
- combine_weights: float32 [768, 2], P('ep'), may hold values from 0.1 to 1
- w_gate: bfloat16 [8, 3072, 8192], P('ep', None, 'tp'), may hold values from -0.21875 to 0.21875
- w_up: bfloat16 [8, 3072, 8192], P('ep', None, 'tp'), may hold values from -0.109375 to 0.109375
- w_down: bfloat16 [8, 8192, 3072], P('ep', 'tp'), may hold values from -0.125 to 0.125
Outputs:
- mixed: bfloat16 [768, 3072], P('ep', 'tp')
- grad_tokens: bfloat16 [768, 3072], P('ep', 'tp')
- grad_combine: float32 [768, 2], P('ep')
- grad_gate: bfloat16 [8, 3072, 8192], P('ep', 'tp')
- grad_up: bfloat16 [8, 3072, 8192], P('ep', 'tp')
- grad_down: bfloat16 [8, 8192, 3072], P('ep', None, 'tp')
Inputs may be any that keep to these rules, and one draw needn't show every extreme that they name: `expert_ids`: each row names 2 different experts. Among the 96 rows of one index of ep, no expert is named more than 40 times, and in some such blocks one expert is named exactly 40 times.
All inputs are finite; a program needn't handle non-finite values.
Results may differ from a plain program's by a relative error of at most 0.019.
Values may be sent and summed in bfloat16 or wider, within the bound.
No kernel may reach another device: no remote copies, remote signals or barrier semaphores. Data moves between devices by JAX's collectives and lax.ppermute only.
A program may use at most 64 MiB of HBM per device.

v0:
```python
import math

import jax
import jax.numpy as jnp
from jax import lax
from jax.experimental import pallas as pl
from jax.experimental.pallas import tpu as pltpu
from jax.sharding import PartitionSpec as P


BF = jnp.bfloat16
F32 = jnp.float32
LIMIT = pltpu.CompilerParams(vmem_limit_bytes=24 * 2**20)


def dot(a, b, ca, cb):
    return lax.dot_general(a, b, (((ca,), (cb,)), ((), ())), preferred_element_type=F32)


def halves(v):
    hi = v.astype(BF)
    return hi, (v - hi.astype(F32)).astype(BF)


def vmem():
    return pl.BlockSpec(memory_space=pltpu.VMEM)


def smem():
    return pl.BlockSpec(memory_space=pltpu.SMEM)


def partials(core, hidden, ggp, gup, wg, wu, wd, chips, width, steps=4):
    rows, hid = hidden.shape
    feats = wg.shape[0]
    block = feats // steps
    each = chips // steps
    lanes = 2 * rows
    pad = 64

    def kernel(core_ref, h_ref, g_ref, u_ref, wg_ref, wu_ref, wd_ref, keep_ref, give_ref, both):
        zeros = jnp.zeros((pad, hid), BF)
        h = jnp.concatenate([h_ref[...], zeros], axis=0)
        g = jnp.concatenate([zeros, g_ref[...]], axis=0)
        u = jnp.concatenate([zeros, u_ref[...]], axis=0)
        out_t = dot(wd_ref[...].T, h, 1, 1)
        in_t = dot(wg_ref[...], g, 1, 1) + dot(wu_ref[...], u, 1, 1)
        mid = rows - pad
        joined = jnp.concatenate(
            [
                out_t[:, :mid],
                out_t[:, mid : mid + 128] + in_t[:, :128],
                in_t[:, 128:],
            ],
            axis=1,
        ).astype(BF)
        both[...] = joined.reshape(each, 2, width, lanes)
        c = core_ref[0]
        for i in range(each):
            keep_ref[i] = both[i, c]
            give_ref[i] = both[i, 1 - c]

    whole = pl.BlockSpec((rows, hid), lambda i: (0, 0))
    out = pl.BlockSpec((each, width, lanes), lambda i: (i, 0, 0))
    return pl.pallas_call(
        kernel,
        grid=(steps,),
        out_shape=[jax.ShapeDtypeStruct((chips, width, lanes), BF)] * 2,
        in_specs=[
            smem(),
            whole,
            whole,
            whole,
            pl.BlockSpec((block, hid), lambda i: (i, 0)),
            pl.BlockSpec((block, hid), lambda i: (i, 0)),
            pl.BlockSpec((hid, block), lambda i: (0, i)),
        ],
        out_specs=[out, out],
        scratch_shapes=[pltpu.VMEM((each, 2, width, lanes), BF)],
        compiler_params=LIMIT,
        name="partials",
    )(core, hidden, ggp, gup, wg, wu, wd)


def add_pair(keep, got, extra, steps=2):
    chips, width, lanes = keep.shape
    more = extra.shape[0]
    each = chips // steps

    def kernel(a, b, e, o):
        o[:, :width] = (a[...].astype(F32) + b[...].astype(F32)).astype(BF)
        for i in range(each):
            o[i, width:] = e[...]

    spec = pl.BlockSpec((each, width, lanes), lambda i: (i, 0, 0))
    return pl.pallas_call(
        kernel,
        grid=(steps,),
        out_shape=jax.ShapeDtypeStruct((chips, width + more, lanes), BF),
        in_specs=[spec, spec, pl.BlockSpec((more, lanes), lambda i: (0, 0))],
        out_specs=pl.BlockSpec((each, width + more, lanes), lambda i: (i, 0, 0)),
        compiler_params=LIMIT,
        name="add_pair",
    )(keep, got, extra)


def extra_rows(v, more):
    hi = v.astype(BF).astype(F32)
    return jnp.concatenate([hi, v - hi, jnp.zeros((more - 2, v.shape[1]), F32)], axis=0)


def finish_sum(parts, width, groups):
    chips, _, lanes = parts.shape
    rows = lanes // 2
    cap = rows // groups

    def kernel(ref, out, turned):
        total = ref[0].astype(F32)
        for i in range(1, chips):
            total += ref[i].astype(F32)
        e = total[width : width + 1] + total[width + 1 : width + 2]
        turned[...] = jnp.concatenate([total[:width], extra_rows(e, 128 - width)], axis=0).T
        for g in range(groups):
            at = g * cap
            out[g] = jnp.concatenate(
                [turned[at : at + cap], turned[rows + at : rows + at + cap]], axis=0
            ).astype(BF)

    return pl.pallas_call(
        kernel,
        out_shape=jax.ShapeDtypeStruct((groups, 2 * cap, 128), BF),
        in_specs=[vmem()],
        out_specs=vmem(),
        scratch_shapes=[pltpu.VMEM((lanes, 128), F32)],
        compiler_params=LIMIT,
        name="finish_sum",
    )(parts)


def assemble(place, mine, theirs):
    side = len(mine)
    wide, lanes = mine[0].shape
    width = wide // side
    chips = side * side

    def kernel(at, *refs):
        full, line = refs[2 * side :]
        x, y, c = at[0], at[1], at[2]

        def chip_of(core, dx, dy):
            across = lax.rem(x + dx + side, side), lax.rem(y + dy + side, side)
            down = lax.rem(x + dy + side, side), lax.rem(y + dx + side, side)
            first = core == 0
            cx = jnp.where(first, across[0], down[0])
            cy = jnp.where(first, across[1], down[1])
            return cy * side + cx

        for q in range(2):
            core = c if q == 0 else 1 - c
            for j in range(side):
                for i in range(side):
                    full[chip_of(core, -i, -j) * 2 + core] = refs[q * side + j][
                        i * width : (i + 1) * width
                    ]
        for q in range(2):
            core = c if q == 0 else 1 - c
            for d in range(side):
                rows = slice((q * side + d) * width, (q * side + d + 1) * width)
                line[rows] = full[chip_of(c, 0, d) * 2 + core]

    return pl.pallas_call(
        kernel,
        out_shape=[
            jax.ShapeDtypeStruct((2 * chips, width, lanes), BF),
            jax.ShapeDtypeStruct((2 * side * width, lanes), BF),
        ],
        in_specs=[smem()] + [vmem()] * (2 * side),
        out_specs=[vmem()] * 2,
        compiler_params=LIMIT,
        name="assemble",
    )(place, *mine, *theirs)


def weight_grads(line, factors, width):
    features, lanes = line.shape
    rows = lanes // 2
    n = len(factors)
    hid = factors[0].shape[1] // 3
    devices = features // width
    pad = 64
    deep = rows + pad

    def kernel(*refs):
        lhs = refs[0]
        fs, outs = refs[1 : 1 + n], refs[1 + n : 1 + n + devices]
        g, h = refs[1 + n + devices :]
        g[rows:] = jnp.zeros((pad, 2 * hid), BF)
        h[:pad] = jnp.zeros((pad, hid), BF)
        for s in range(n):
            g[:rows] = fs[s][:, : 2 * hid]
            h[pad:] = fs[s][:, 2 * hid :]
            rg = dot(lhs[:, :deep], g[...], 1, 0).astype(BF)
            rh = dot(lhs[:, lanes - deep :], h[...], 1, 0).astype(BF)
            for j in range(devices):
                at = slice(j * width, (j + 1) * width)
                o = s * 3 * hid
                outs[j][:, o : o + 2 * hid] = rg[at]
                outs[j][:, o + 2 * hid : o + 3 * hid] = rh[at]

    return pl.pallas_call(
        kernel,
        out_shape=[jax.ShapeDtypeStruct((width, n * 3 * hid), BF)] * devices,
        in_specs=[vmem()] * (1 + n),
        out_specs=[vmem()] * devices,
        scratch_shapes=[pltpu.VMEM((deep, 2 * hid), BF), pltpu.VMEM((deep, hid), BF)],
        compiler_params=LIMIT,
        name="weight_grads",
    )(line, *factors)


def lay_out(columns, pieces, hid, steps=3):
    width, wide = pieces[0].shape
    n = len(pieces)
    per = wide // (3 * hid)
    total = n * per * hid
    block = width // steps

    def kernel(cols, *refs):
        ins, outs = refs[:n], refs[n:]
        for p in range(n):
            for s in range(per):
                at = pl.multiple_of(cols[p * per + s], hid)
                for m in range(3):
                    o = (s * 3 + m) * hid
                    outs[m][:, pl.ds(at, hid)] = ins[p][:, o : o + hid]

    return pl.pallas_call(
        kernel,
        grid=(steps,),
        out_shape=[jax.ShapeDtypeStruct((width, total), BF)] * 3,
        in_specs=[smem()] + [pl.BlockSpec((block, wide), lambda i: (i, 0))] * n,
        out_specs=[pl.BlockSpec((block, total), lambda i: (i, 0))] * 3,
        compiler_params=LIMIT,
        name="lay_out",
    )(columns, *pieces)


def body(tokens, cotangent, expert_ids, combine_weights, w_gate, w_up, w_down):
    groups = lax.axis_size("ep")
    devices = lax.axis_size("tp")
    chips = devices // 2
    tok_rows, width = tokens.shape
    chosen = expert_ids.shape[1]
    cap = tok_rows * chosen * 5 // (3 * groups)
    rows = groups * cap
    wg, wu, wd = w_gate[0], w_up[0], w_down[0]
    hid = wg.shape[1]
    feats = wg.shape[0]
    side = math.isqrt(chips)
    here = lax.axis_index("tp")
    core, cx, cy = here % 2, here // 2 % side, here // (2 * side)
    swap = [(i, i ^ 1) for i in range(devices)]

    def along(v, d, turn=0, other=0):
        pairs = []
        for y in range(side):
            for x in range(side):
                for c in range(2):
                    dx, dy = (d, 0) if c == turn else (0, d)
                    to = ((y + dy) % side * side + (x + dx) % side) * 2 + (c ^ other)
                    pairs.append(((y * side + x) * 2 + c, to))
        return lax.ppermute(v, "tp", pairs)

    def swapped(v):
        return lax.ppermute(v, "tp", swap)

    ids = [expert_ids[:, k] for k in range(chosen)]
    hot = [
        (i[:, None] == jnp.arange(groups, dtype=jnp.int32)[None, :]).astype(F32) for i in ids
    ]
    both = sum(hot)
    t = jnp.arange(tok_rows, dtype=jnp.int32)
    before = jnp.dot((t[:, None] > t[None, :]).astype(F32), both)
    place = []
    for k in range(chosen):
        rank = jnp.sum(before * hot[k], axis=1).astype(jnp.int32)
        slot = ids[k] * cap + rank
        place.append((slot[None, :] == jnp.arange(rows, dtype=jnp.int32)[:, None]).astype(BF))
    cot = cotangent.astype(F32)
    weight = [combine_weights[:, k][:, None] for k in range(chosen)]
    send_rows = dot(sum(place), tokens, 1, 0)
    send_grad = sum(dot(place[k], (weight[k] * cot).astype(BF), 1, 0) for k in range(chosen))
    send = jnp.concatenate(
        [send_rows.reshape(groups, cap, width), send_grad.reshape(groups, cap, width)], axis=1
    ).astype(BF)
    recv = lax.all_to_all(send, "ep", 0, 0, tiled=True)
    piece = (
        jnp.concatenate(
            [recv[:, :cap].reshape(rows, width), recv[:, cap:].reshape(rows, width)], axis=0
        )
    ).T

    place_now = jnp.stack([cx, cy, core])
    steps = (1, 3, 2) if side == 4 else range(1, side)
    order = (0, *steps)

    def line_of(v, turn):
        got = {0: v, **{d: along(v, d, turn) for d in steps}}
        return [got[d] for d in range(side)]

    mine = line_of(jnp.concatenate(line_of(piece, 0)), 1)
    theirs = {d: swapped(mine[d]) for d in order}
    full, line = assemble(place_now, mine, [theirs[d] for d in range(side)])
    full = full.reshape(feats, 2 * rows)
    x, dy = full[:, :rows], full[:, rows:]

    gate_pre = dot(x, wg, 0, 0)
    up_pre = dot(x, wu, 0, 0)
    sigma = jax.nn.sigmoid(gate_pre)
    active = gate_pre * sigma
    slope = sigma * (1.0 + gate_pre * (1.0 - sigma))
    hidden = (active * up_pre).astype(BF)
    grad_hidden = dot(dy, wd, 0, 1)
    ggp = (grad_hidden * up_pre * slope).astype(BF)
    gup = (grad_hidden * active).astype(BF)
    inner = jnp.sum(hidden.astype(F32) * grad_hidden, axis=1)

    factors = line_of(jnp.concatenate([ggp, gup, hidden], axis=1), 0)

    keep, give = partials(core[None], hidden, ggp, gup, wg, wu, wd, chips, width)
    got = swapped(give)
    inner = inner + swapped(inner)
    hi, lo = halves(inner)
    more = 8
    extra = jnp.pad(jnp.stack([hi, lo]), ((0, more - 2), (0, rows)))
    reduced = add_pair(keep, got, extra)
    same_core = [[2 * i + c for i in range(chips)] for c in range(2)]
    parts = lax.all_to_all(
        reduced, "tp", 0, 0, tiled=True, axis_index_groups=same_core
    )
    back = finish_sum(parts, width, groups)

    grads = weight_grads(line, factors, width)
    pieces = {(0, 0): grads[0]}
    for d in (*steps, 0):
        for q in range(2):
            if (q, d) != (0, 0):
                pieces[q, d] = along(grads[q * side + d], d, 1, q)
    r = jnp.arange(side)
    columns = []
    for q in range(2):
        sender = core ^ q
        for d in range(side):
            fx, fy = (cx - r) % side, (cy - d) % side
            tx, ty = (cx - d) % side, (cy - r) % side
            chip = jnp.where(sender == 0, fy * side + fx, ty * side + tx)
            columns.append((chip * 2 + sender) * hid)
    columns = jnp.concatenate(columns)
    pieces = [pieces[q, d] for q in range(2) for d in range(side)]

    back = lax.all_to_all(back, "ep", 0, 0, tiled=True)
    out_back = back[:, :cap].reshape(rows, -1)
    in_back = back[:, cap:].reshape(rows, -1)
    chosen_out = [dot(place[k], out_back, 0, 0) for k in range(chosen)]
    mixed = sum(weight[k] * chosen_out[k][:, :width] for k in range(chosen)).astype(BF)
    grad_combine = jnp.concatenate(
        [
            (chosen_out[k][:, width : width + 1] + chosen_out[k][:, width + 1 : width + 2])
            / weight[k]
            for k in range(chosen)
        ],
        axis=1,
    )
    grad_tokens = dot(sum(place), in_back[:, :width], 0, 0).astype(BF)

    gate_out, up_out, down_out = lay_out(columns, pieces, hid)
    return (
        mixed,
        grad_tokens,
        grad_combine,
        gate_out[None],
        up_out[None],
        down_out.T[None],
    )


def solution(mesh):
    return jax.shard_map(
        body,
        mesh=mesh,
        in_specs=(
            P("ep", "tp"),
            P("ep", "tp"),
            P("ep", None),
            P("ep", None),
            P("ep", None, "tp"),
            P("ep", None, "tp"),
            P("ep", "tp", None),
        ),
        out_specs=(
            P("ep", "tp"),
            P("ep", "tp"),
            P("ep", None),
            P("ep", "tp", None),
            P("ep", "tp", None),
            P("ep", None, "tp"),
        ),
        check_vma=False,
    )
```

profile of v0, /device:TPU:1, one launch (start us, length us, event | category | flops | bytes accessed | tf_op | source)
XLA Modules:
  0.0 168.0 jit_solution(16250297488036402845)
XLA Ops:
  5.6 17.0 %all_to_all.15 = bf16[8,80,96]{2,1,0:T(8,128)(2,1)S(1)} all-to-all(bf16[8,80,96]{2,1,0:T(8,128)(2,1)S(1)} %pad_maximum_fusion.2), channel_id=1, replica_groups=mesh['ep'=8,'tp'=32] {'ep'}, dimensions={0} | all-to-all | bytes 245760 | tf_op jit(solution)/shard_map/all_to_all | solution.py:296
  23.0 2.8 %collective-permute-start.2 = (bf16[96,640]{1,0:T(8,128)(2,1)S(1)}, bf16[96,640]{1,0:T(8,128)(2,1)S(1)}, u32[]{:S(2)}, u32[]{:S(2)}) collective-permute-start(bf16[96,640]{1,0:T(8,128)(2,1)S(1)} %maximum_bitcast_fusion), channel_id=1, source_target_pairs={{0,6},{1,25},{2,0},{3,27},{4,2},{5,29},{6,4},{7,31},{8,14},{9,1},{... | collective-permute-start | bytes 368648 | tf_op jit(solution)/shard_map/ppermute | solution.py:272
  26.9 2.1 %collective-permute-done.2 = bf16[96,640]{1,0:T(8,128)(2,1)S(1)} collective-permute-done((bf16[96,640]{1,0:T(8,128)(2,1)S(1)}, bf16[96,640]{1,0:T(8,128)(2,1)S(1)}, u32[]{:S(2)}, u32[]{:S(2)}) %collective-permute-start.2) | collective-permute-done | bytes 122912 | tf_op jit(solution)/shard_map/ppermute | solution.py:272
  29.0 2.2 %collective-permute-done.1 = bf16[96,640]{1,0:T(8,128)(2,1)S(1)} collective-permute-done((bf16[96,640]{1,0:T(8,128)(2,1)S(1)}, bf16[96,640]{1,0:T(8,128)(2,1)S(1)}, u32[]{:S(2)}, u32[]{:S(2)}) %collective-permute-start.1) | collective-permute-done | bytes 122912 | tf_op jit(solution)/shard_map/ppermute | solution.py:272
  33.7 2.7 %collective-permute-start.4 = (bf16[384,640]{1,0:T(8,128)(2,1)S(1)}, bf16[384,640]{1,0:T(8,128)(2,1)S(1)}, u32[]{:S(2)}, u32[]{:S(2)}) collective-permute-start(bf16[384,640]{1,0:T(8,128)(2,1)S(1)} %pad_maximum_fusion.refs_0_), channel_id=1, source_target_pairs={{0,16},{1,5},{2,18},{3,7},{4,20},{5,1},{6,22},{7,3},{8,24},{9,13},... | collective-permute-start | bytes 1474568 | tf_op jit(solution)/shard_map/ppermute | solution.py:272
  37.3 5.9 %collective-permute-start.6 = (bf16[384,640]{1,0:T(8,128)(2,1)S(1)}, bf16[384,640]{1,0:T(8,128)(2,1)}, u32[]{:S(2)}, u32[]{:S(2)}) collective-permute-start(bf16[384,640]{1,0:T(8,128)(2,1)S(1)} %pad_maximum_fusion.refs_0_), channel_id=1, source_target_pairs={{0,1},{1,0},{2,3},{3,2},{4,5},{5,4},{6,7},{7,6},{8,9},{9,8},{10,11... | collective-permute-start | bytes 1474568 | tf_op jit(solution)/shard_map/ppermute | solution.py:275
  43.3 4.0 %collective-permute-start.7 = (bf16[384,640]{1,0:T(8,128)(2,1)S(1)}, bf16[384,640]{1,0:T(8,128)(2,1)}, u32[]{:S(2)}, u32[]{:S(2)}) collective-permute-start(bf16[384,640]{1,0:T(8,128)(2,1)S(1)} %collective-permute-done.3.refs_1_), channel_id=1, source_target_pairs={{0,1},{1,0},{2,3},{3,2},{4,5},{5,4},{6,7},{7,6},{8,9},{9,8},{10,11... | collective-permute-start | bytes 1474568 | tf_op jit(solution)/shard_map/ppermute | solution.py:275
  48.1 5.9 %collective-permute-start.8 = (bf16[384,640]{1,0:T(8,128)(2,1)S(1)}, bf16[384,640]{1,0:T(8,128)(2,1)}, u32[]{:S(2)}, u32[]{:S(2)}) collective-permute-start(bf16[384,640]{1,0:T(8,128)(2,1)S(1)} %collective-permute-done.4.refs_2_), channel_id=1, source_target_pairs={{0,1},{1,0},{2,3},{3,2},{4,5},{5,4},{6,7},{7,6},{8,9},{9,8},{10,11... | collective-permute-start | bytes 1474568 | tf_op jit(solution)/shard_map/ppermute | solution.py:275
  55.6 1.4 collective-permute-done.9.refs_7_
  59.0 2.0 %assemble.1 = (bf16[32,96,640]{2,1,0:T(8,128)(2,1)S(1)}, bf16[768,640]{1,0:T(8,128)(2,1)S(1)}) custom-call(s32[3]{0:T(128)S(1)} %pad_add_fusion.at, bf16[384,640]{1,0:T(8,128)(2,1)S(1)} %pad_maximum_fusion.refs_0_, bf16[384,640]{1,0:T(8,128)(2,1)S(1)} %copy-done.11, bf16[384,640]{1,0:T(8,128)(2,1)S(1)} %copy-done.13, ...), custom_call_target="tpu_custom_call" | custom-call | tf_op jit(solution)/shard_map/assemble/pallas_call | solution.py:171
  63.9 1.7 %multiply_reduce_fusion = (f32[320]{0:T(512)S(1)}, bf16[320,256]{1,0:T(8,128)(2,1)S(1)}, bf16[320,256]{1,0:T(8,128)(2,1)S(1)}, bf16[320,256]{1,0:T(8,128)(2,1)S(1)}) fusion(f32[320,256]{1,0:T(8,128)S(1)} %fusion.2, f32[320,256]{1,0:T(8,128)S(1)} %fusion.4, bf16[1,256,3072]{2,1,0:T(8,128)(2,1)S(1)} %copy-done.4, bf16[3072,640]{1,0:T(8,128)(2,1)S(1)} %bitcast.48), kind=kOutput, calls=%fused_computation.12 | convolution fusion | flops 504790720 | bytes 5080320 | tf_op jit(solution)/shard_map/dot_general | solution.py:17
  65.6 3.8 %partials.1 = (bf16[16,96,640]{2,1,0:T(8,128)(2,1)S(1)}, bf16[16,96,640]{2,1,0:T(8,128)(2,1)S(1)}) custom-call(s32[1]{0:T(128)} %bitcast.2.core_ref, bf16[320,256]{1,0:T(8,128)(2,1)S(1)} %get-tuple-element.51.h_ref, bf16[320,256]{1,0:T(8,128)(2,1)S(1)} %get-tuple-element.52.g_ref, bf16[320,256]{1,0:T(8,128)(2,1)S(1)} %get-tuple-element.53.u_ref, ...), custom_call_target="tpu_custom_call" | custom-call | tf_op jit(solution)/shard_map/partials/pallas_call | solution.py:65
  70.2 3.5 %collective-permute-done.11 = f32[320]{0:T(512)S(1)} collective-permute-done((f32[320]{0:T(512)S(1)}, f32[320]{0:T(512)S(1)}, u32[]{:S(2)}, u32[]{:S(2)}) %collective-permute-start.11) | collective-permute-done | bytes 1312 | tf_op jit(solution)/shard_map/ppermute | solution.py:275
  75.6 3.7 %all-to-all-start.1 = ((bf16[16,104,640]{2,1,0:T(8,128)(2,1)}), bf16[16,104,640]{2,1,0:T(8,128)(2,1)S(1)}, u32[]{:S(2)}, u32[]{:S(2)}) async-start(bf16[16,104,640]{2,1,0:T(8,128)(2,1)} %copy-done.1), calls=%async_computation.1 | async-start | bytes 4259840 | tf_op jit(solution)/shard_map/all_to_all | solution.py:338
  81.6 2.4 %collective-permute-start.13 = (bf16[320,768]{1,0:T(8,128)(2,1)S(1)}, bf16[320,768]{1,0:T(8,128)(2,1)S(1)}, u32[]{:S(2)}, u32[]{:S(2)}) collective-permute-start(bf16[320,768]{1,0:T(8,128)(2,1)S(1)} %pad_maximum_fusion.1.refs_1_), channel_id=1, source_target_pairs={{0,4},{1,17},{2,6},{3,19},{4,0},{5,21},{6,2},{7,23},{8,12},{9,25},... | collective-permute-start | bytes 1474568 | tf_op jit(solution)/shard_map/ppermute | solution.py:272
  85.2 23.3 %collective-permute-done.12.refs_2_ = bf16[320,768]{1,0:T(8,128)(2,1)S(1)} collective-permute-done((bf16[320,768]{1,0:T(8,128)(2,1)S(1)}, bf16[320,768]{1,0:T(8,128)(2,1)S(1)}, u32[]{:S(2)}, u32[]{:S(2)}) %collective-permute-start.12) | collective-permute-done | bytes 491552 | tf_op jit(solution)/shard_map/ppermute | solution.py:272
  108.5 8.1 %collective-permute-done.13.refs_3_ = bf16[320,768]{1,0:T(8,128)(2,1)S(1)} collective-permute-done((bf16[320,768]{1,0:T(8,128)(2,1)S(1)}, bf16[320,768]{1,0:T(8,128)(2,1)S(1)}, u32[]{:S(2)}, u32[]{:S(2)}) %collective-permute-start.13) | collective-permute-done | bytes 491552 | tf_op jit(solution)/shard_map/ppermute | solution.py:272
  116.6 4.1 %weight_grads.1 = (bf16[96,3072]{1,0:T(8,128)(2,1)S(1)}, bf16[96,3072]{1,0:T(8,128)(2,1)S(1)}, bf16[96,3072]{1,0:T(8,128)(2,1)S(1)}, bf16[96,3072]{1,0:T(8,128)(...) custom-call(bf16[768,640]{1,0:T(8,128)(2,1)S(1)} %get-tuple-element., ...), custom_call_target="tpu_custom_call" | custom-call | tf_op jit(solution)/shard_map/weight_grads/pallas_call | solution.py:210
  122.7 2.7 %collective-permute-start.16 = (bf16[96,3072]{1,0:T(8,128)(2,1)S(1)}, bf16[96,3072]{1,0:T(8,128)(2,1)S(1)}, u32[]{:S(2)}, u32[]{:S(2)}) collective-permute-start(bf16[96,3072]{1,0:T(8,128)(2,1)S(1)} %get-tuple-element.27), channel_id=1, source_target_pairs={{0,16},{1,5},{2,18},{3,7},{4,20},{5,1},{6,22},{7,3},{8,24},{9,13},... | collective-permute-start | bytes 1769480 | tf_op jit(solution)/shard_map/ppermute | solution.py:272
  126.3 7.8 %collective-permute-start.18 = (bf16[96,3072]{1,0:T(8,128)(2,1)}, bf16[96,3072]{1,0:T(8,128)(2,1)}, u32[]{:S(2)}, u32[]{:S(2)}) collective-permute-start(bf16[96,3072]{1,0:T(8,128)(2,1)} %get-tuple-element.29), channel_id=1, source_target_pairs={{0,1},{1,0},{2,3},{3,2},{4,5},{5,4},{6,7},{7,6},{8,9},{9,8},{10,11... | collective-permute-start | bytes 1769480 | tf_op jit(solution)/shard_map/ppermute | solution.py:272
  134.1 11.7 %collective-permute-start.20 = (bf16[96,3072]{1,0:T(8,128)(2,1)}, bf16[96,3072]{1,0:T(8,128)(2,1)}, u32[]{:S(2)}, u32[]{:S(2)}) collective-permute-start(bf16[96,3072]{1,0:T(8,128)(2,1)} %get-tuple-element.31), channel_id=1, source_target_pairs={{0,17},{1,4},{2,19},{3,6},{4,21},{5,0},{6,23},{7,2},{8,25},{9,12},... | collective-permute-start | bytes 1769480 | tf_op jit(solution)/shard_map/ppermute | solution.py:272
  148.0 3.4 %all-to-all-start.2 = ((bf16[8,80,128]{2,1,0:T(8,128)(2,1)}), bf16[8,80,128]{2,1,0:T(8,128)(2,1)S(1)}, u32[]{:S(2)}, u32[]{:S(2)}) async-start(bf16[8,80,128]{2,1,0:T(8,128)(2,1)} %finish_sum.1), calls=%async_computation.2 | async-start | bytes 327680 | tf_op jit(solution)/shard_map/all_to_all | solution.py:361
  152.0 6.3 %collective-permute-done.20.refs_6_ = bf16[96,3072]{1,0:T(8,128)(2,1)} collective-permute-done((bf16[96,3072]{1,0:T(8,128)(2,1)}, bf16[96,3072]{1,0:T(8,128)(2,1)}, u32[]{:S(2)}, u32[]{:S(2)}) %collective-permute-start.20) | collective-permute-done | bytes 589856 | tf_op jit(solution)/shard_map/ppermute | solution.py:272
  160.2 4.9 %lay_out.1 = (bf16[96,8192]{1,0:T(8,128)(2,1)}, bf16[96,8192]{1,0:T(8,128)(2,1)}, bf16[96,8192]{1,0:T(8,128)(2,1)}) custom-call(s32[32]{0:T(128)S(1)} %concatenate.23.cols, bf16[96,3072]{1,0:T(8,128)(2,1)S(1)} %copy-done.7, bf16[96,3072]{1,0:T(8,128)(2,1)S(1)} %collective-permute-done.15.refs_1_, bf16[96,3072]{1,0:T(8,128)(2,1)S(1)} %copy-done.9, ...), custom_call_target="tpu_custom_call" | custom-call | tf_op jit(solution)/shard_map/lay_out/pallas_call | solution.py:237
  (100 shorter events, 33.7 us)
Async XLA Ops:
  23.0 6.0 %collective-permute-start.2 = (bf16[96,640]{1,0:T(8,128)(2,1)S(1)}, bf16[96,640]{1,0:T(8,128)(2,1)S(1)}, u32[]{:S(2)}, u32[]{:S(2)}) collective-permute-start(bf16[96,640]{1,0:T(8,128)(2,1)S(1)} %maximum_bitcast_fusion), channel_id=1, source_target_pairs={{0,6},{1,25},{2,0},{3,27},{4,2},{5,29},{6,4},{7,31},{8,14},{9,1},{... | collective-permute-start | bytes 368648 | tf_op jit(solution)/shard_map/ppermute | solution.py:272
  25.8 5.3 %collective-permute-start.1 = (bf16[96,640]{1,0:T(8,128)(2,1)S(1)}, bf16[96,640]{1,0:T(8,128)(2,1)S(1)}, u32[]{:S(2)}, u32[]{:S(2)}) collective-permute-start(bf16[96,640]{1,0:T(8,128)(2,1)S(1)} %maximum_bitcast_fusion), channel_id=1, source_target_pairs={{0,4},{1,17},{2,6},{3,19},{4,0},{5,21},{6,2},{7,23},{8,12},{9,25},... | collective-permute-start | bytes 368648 | tf_op jit(solution)/shard_map/ppermute | solution.py:272
  26.2 6.2 %collective-permute-start = (bf16[96,640]{1,0:T(8,128)(2,1)S(1)}, bf16[96,640]{1,0:T(8,128)(2,1)S(1)}, u32[]{:S(2)}, u32[]{:S(2)}) collective-permute-start(bf16[96,640]{1,0:T(8,128)(2,1)S(1)} %maximum_bitcast_fusion), channel_id=1, source_target_pairs={{0,2},{1,9},{2,4},{3,11},{4,6},{5,13},{6,0},{7,15},{8,10},{9,17},{... | collective-permute-start | bytes 368648 | tf_op jit(solution)/shard_map/ppermute | solution.py:272
  32.4 10.8 %collective-permute-start.3 = (bf16[384,640]{1,0:T(8,128)(2,1)S(1)}, bf16[384,640]{1,0:T(8,128)(2,1)S(1)}, u32[]{:S(2)}, u32[]{:S(2)}) collective-permute-start(bf16[384,640]{1,0:T(8,128)(2,1)S(1)} %pad_maximum_fusion.refs_0_), channel_id=1, source_target_pairs={{0,8},{1,3},{2,10},{3,5},{4,12},{5,7},{6,14},{7,1},{8,16},{9,11},{... | collective-permute-start | bytes 1474568 | tf_op jit(solution)/shard_map/ppermute | solution.py:272
  33.7 14.3 %collective-permute-start.4 = (bf16[384,640]{1,0:T(8,128)(2,1)S(1)}, bf16[384,640]{1,0:T(8,128)(2,1)S(1)}, u32[]{:S(2)}, u32[]{:S(2)}) collective-permute-start(bf16[384,640]{1,0:T(8,128)(2,1)S(1)} %pad_maximum_fusion.refs_0_), channel_id=1, source_target_pairs={{0,16},{1,5},{2,18},{3,7},{4,20},{5,1},{6,22},{7,3},{8,24},{9,13},... | collective-permute-start | bytes 1474568 | tf_op jit(solution)/shard_map/ppermute | solution.py:272
  36.4 18.4 %collective-permute-start.5 = (bf16[384,640]{1,0:T(8,128)(2,1)S(1)}, bf16[384,640]{1,0:T(8,128)(2,1)}, u32[]{:S(2)}, u32[]{:S(2)}) collective-permute-start(bf16[384,640]{1,0:T(8,128)(2,1)S(1)} %pad_maximum_fusion.refs_0_), channel_id=1, source_target_pairs={{0,24},{1,7},{2,26},{3,1},{4,28},{5,3},{6,30},{7,5},{8,0},{9,15},{... | collective-permute-start | bytes 1474568 | tf_op jit(solution)/shard_map/ppermute | solution.py:272
  37.3 17.5 %collective-permute-start.6 = (bf16[384,640]{1,0:T(8,128)(2,1)S(1)}, bf16[384,640]{1,0:T(8,128)(2,1)}, u32[]{:S(2)}, u32[]{:S(2)}) collective-permute-start(bf16[384,640]{1,0:T(8,128)(2,1)S(1)} %pad_maximum_fusion.refs_0_), channel_id=1, source_target_pairs={{0,1},{1,0},{2,3},{3,2},{4,5},{5,4},{6,7},{7,6},{8,9},{9,8},{10,11... | collective-permute-start | bytes 1474568 | tf_op jit(solution)/shard_map/ppermute | solution.py:275
  43.3 11.6 %collective-permute-start.7 = (bf16[384,640]{1,0:T(8,128)(2,1)S(1)}, bf16[384,640]{1,0:T(8,128)(2,1)}, u32[]{:S(2)}, u32[]{:S(2)}) collective-permute-start(bf16[384,640]{1,0:T(8,128)(2,1)S(1)} %collective-permute-done.3.refs_1_), channel_id=1, source_target_pairs={{0,1},{1,0},{2,3},{3,2},{4,5},{5,4},{6,7},{7,6},{8,9},{9,8},{10,11... | collective-permute-start | bytes 1474568 | tf_op jit(solution)/shard_map/ppermute | solution.py:275
  48.1 7.6 %collective-permute-start.8 = (bf16[384,640]{1,0:T(8,128)(2,1)S(1)}, bf16[384,640]{1,0:T(8,128)(2,1)}, u32[]{:S(2)}, u32[]{:S(2)}) collective-permute-start(bf16[384,640]{1,0:T(8,128)(2,1)S(1)} %collective-permute-done.4.refs_2_), channel_id=1, source_target_pairs={{0,1},{1,0},{2,3},{3,2},{4,5},{5,4},{6,7},{7,6},{8,9},{9,8},{10,11... | collective-permute-start | bytes 1474568 | tf_op jit(solution)/shard_map/ppermute | solution.py:275
  54.8 2.2 %collective-permute-start.9 = (bf16[384,640]{1,0:T(8,128)(2,1)}, bf16[384,640]{1,0:T(8,128)(2,1)}, u32[]{:S(2)}, u32[]{:S(2)}) collective-permute-start(bf16[384,640]{1,0:T(8,128)(2,1)} %collective-permute-done.5.refs_3_), channel_id=1, source_target_pairs={{0,1},{1,0},{2,3},{3,2},{4,5},{5,4},{6,7},{7,6},{8,9},{9,8},{10,11... | collective-permute-start | bytes 1474568 | tf_op jit(solution)/shard_map/ppermute | solution.py:275
  69.4 4.3 %collective-permute-start.10 = (bf16[16,96,640]{2,1,0:T(8,128)(2,1)S(1)}, bf16[16,96,640]{2,1,0:T(8,128)(2,1)S(1)}, u32[]{:S(2)}, u32[]{:S(2)}) collective-permute-start(bf16[16,96,640]{2,1,0:T(8,128)(2,1)S(1)} %get-tuple-element.23), channel_id=1, source_target_pairs={{0,1},{1,0},{2,3},{3,2},{4,5},{5,4},{6,7},{7,6},{8,9},{9,8},{10,11... | collective-permute-start | bytes 5898248 | tf_op jit(solution)/shard_map/ppermute | solution.py:275
  69.8 3.8 %collective-permute-start.11 = (f32[320]{0:T(512)S(1)}, f32[320]{0:T(512)S(1)}, u32[]{:S(2)}, u32[]{:S(2)}) collective-permute-start(f32[320]{0:T(512)S(1)} %get-tuple-element.50), channel_id=1, source_target_pairs={{0,1},{1,0},{2,3},{3,2},{4,5},{5,4},{6,7},{7,6},{8,9},{9,8},{10,11... | collective-permute-start | bytes 3848 | tf_op jit(solution)/shard_map/ppermute | solution.py:275
  75.6 71.3 %all-to-all-start.1 = ((bf16[16,104,640]{2,1,0:T(8,128)(2,1)}), bf16[16,104,640]{2,1,0:T(8,128)(2,1)S(1)}, u32[]{:S(2)}, u32[]{:S(2)}) async-start(bf16[16,104,640]{2,1,0:T(8,128)(2,1)} %copy-done.1), calls=%async_computation.1 | async-start | bytes 4259840 | tf_op jit(solution)/shard_map/all_to_all | solution.py:338
  80.3 28.3 %collective-permute-start.12 = (bf16[320,768]{1,0:T(8,128)(2,1)S(1)}, bf16[320,768]{1,0:T(8,128)(2,1)S(1)}, u32[]{:S(2)}, u32[]{:S(2)}) collective-permute-start(bf16[320,768]{1,0:T(8,128)(2,1)S(1)} %pad_maximum_fusion.1.refs_1_), channel_id=1, source_target_pairs={{0,2},{1,9},{2,4},{3,11},{4,6},{5,13},{6,0},{7,15},{8,10},{9,17},{... | collective-permute-start | bytes 1474568 | tf_op jit(solution)/shard_map/ppermute | solution.py:272
  81.6 35.0 %collective-permute-start.13 = (bf16[320,768]{1,0:T(8,128)(2,1)S(1)}, bf16[320,768]{1,0:T(8,128)(2,1)S(1)}, u32[]{:S(2)}, u32[]{:S(2)}) collective-permute-start(bf16[320,768]{1,0:T(8,128)(2,1)S(1)} %pad_maximum_fusion.1.refs_1_), channel_id=1, source_target_pairs={{0,4},{1,17},{2,6},{3,19},{4,0},{5,21},{6,2},{7,23},{8,12},{9,25},... | collective-permute-start | bytes 1474568 | tf_op jit(solution)/shard_map/ppermute | solution.py:272
  84.1 32.6 %collective-permute-start.14 = (bf16[320,768]{1,0:T(8,128)(2,1)S(1)}, bf16[320,768]{1,0:T(8,128)(2,1)S(1)}, u32[]{:S(2)}, u32[]{:S(2)}) collective-permute-start(bf16[320,768]{1,0:T(8,128)(2,1)S(1)} %pad_maximum_fusion.1.refs_1_), channel_id=1, source_target_pairs={{0,6},{1,25},{2,0},{3,27},{4,2},{5,29},{6,4},{7,31},{8,14},{9,1},{... | collective-permute-start | bytes 1474568 | tf_op jit(solution)/shard_map/ppermute | solution.py:272
  121.5 12.5 %collective-permute-start.15 = (bf16[96,3072]{1,0:T(8,128)(2,1)S(1)}, bf16[96,3072]{1,0:T(8,128)(2,1)S(1)}, u32[]{:S(2)}, u32[]{:S(2)}) collective-permute-start(bf16[96,3072]{1,0:T(8,128)(2,1)S(1)} %get-tuple-element.26), channel_id=1, source_target_pairs={{0,8},{1,3},{2,10},{3,5},{4,12},{5,7},{6,14},{7,1},{8,16},{9,11},{... | collective-permute-start | bytes 1769480 | tf_op jit(solution)/shard_map/ppermute | solution.py:272
  122.7 23.0 %collective-permute-start.16 = (bf16[96,3072]{1,0:T(8,128)(2,1)S(1)}, bf16[96,3072]{1,0:T(8,128)(2,1)S(1)}, u32[]{:S(2)}, u32[]{:S(2)}) collective-permute-start(bf16[96,3072]{1,0:T(8,128)(2,1)S(1)} %get-tuple-element.27), channel_id=1, source_target_pairs={{0,16},{1,5},{2,18},{3,7},{4,20},{5,1},{6,22},{7,3},{8,24},{9,13},... | collective-permute-start | bytes 1769480 | tf_op jit(solution)/shard_map/ppermute | solution.py:272
  125.4 26.1 %collective-permute-start.17 = (bf16[96,3072]{1,0:T(8,128)(2,1)}, bf16[96,3072]{1,0:T(8,128)(2,1)}, u32[]{:S(2)}, u32[]{:S(2)}) collective-permute-start(bf16[96,3072]{1,0:T(8,128)(2,1)} %get-tuple-element.28), channel_id=1, source_target_pairs={{0,24},{1,7},{2,26},{3,1},{4,28},{5,3},{6,30},{7,5},{8,0},{9,15},{... | collective-permute-start | bytes 1769480 | tf_op jit(solution)/shard_map/ppermute | solution.py:272
  126.3 25.2 %collective-permute-start.18 = (bf16[96,3072]{1,0:T(8,128)(2,1)}, bf16[96,3072]{1,0:T(8,128)(2,1)}, u32[]{:S(2)}, u32[]{:S(2)}) collective-permute-start(bf16[96,3072]{1,0:T(8,128)(2,1)} %get-tuple-element.29), channel_id=1, source_target_pairs={{0,1},{1,0},{2,3},{3,2},{4,5},{5,4},{6,7},{7,6},{8,9},{9,8},{10,11... | collective-permute-start | bytes 1769480 | tf_op jit(solution)/shard_map/ppermute | solution.py:272
  134.1 17.9 %collective-permute-start.19 = (bf16[96,3072]{1,0:T(8,128)(2,1)}, bf16[96,3072]{1,0:T(8,128)(2,1)}, u32[]{:S(2)}, u32[]{:S(2)}) collective-permute-start(bf16[96,3072]{1,0:T(8,128)(2,1)} %get-tuple-element.30), channel_id=1, source_target_pairs={{0,9},{1,2},{2,11},{3,4},{4,13},{5,6},{6,15},{7,0},{8,17},{9,10},{... | collective-permute-start | bytes 1769480 | tf_op jit(solution)/shard_map/ppermute | solution.py:272
  134.1 24.3 %collective-permute-start.20 = (bf16[96,3072]{1,0:T(8,128)(2,1)}, bf16[96,3072]{1,0:T(8,128)(2,1)}, u32[]{:S(2)}, u32[]{:S(2)}) collective-permute-start(bf16[96,3072]{1,0:T(8,128)(2,1)} %get-tuple-element.31), channel_id=1, source_target_pairs={{0,17},{1,4},{2,19},{3,6},{4,21},{5,0},{6,23},{7,2},{8,25},{9,12},... | collective-permute-start | bytes 1769480 | tf_op jit(solution)/shard_map/ppermute | solution.py:272
  146.6 12.5 %collective-permute-start.21 = (bf16[96,3072]{1,0:T(8,128)(2,1)}, bf16[96,3072]{1,0:T(8,128)(2,1)}, u32[]{:S(2)}, u32[]{:S(2)}) collective-permute-start(bf16[96,3072]{1,0:T(8,128)(2,1)} %get-tuple-element.32), channel_id=1, source_target_pairs={{0,25},{1,6},{2,27},{3,0},{4,29},{5,2},{6,31},{7,4},{8,1},{9,14},{... | collective-permute-start | bytes 1769480 | tf_op jit(solution)/shard_map/ppermute | solution.py:272
  148.0 17.1 %all-to-all-start.2 = ((bf16[8,80,128]{2,1,0:T(8,128)(2,1)}), bf16[8,80,128]{2,1,0:T(8,128)(2,1)S(1)}, u32[]{:S(2)}, u32[]{:S(2)}) async-start(bf16[8,80,128]{2,1,0:T(8,128)(2,1)} %finish_sum.1), calls=%async_computation.2 | async-start | bytes 327680 | tf_op jit(solution)/shard_map/all_to_all | solution.py:361
  (14 other events, 62.7 us)
where the time goes:
time: 169 us; the launch traced here: 168 us
  starting transfers between devices  61.7 us (37%)
  waiting for transfers between devices  50.1 us (30%)
  blocking collectives  17 us (10%)
  Pallas kernels  16.3 us (10%)
  local copies, waits for them, and re-layouts  11.3 us (7%)
  matrix products  7.02 us (4%)
  other arithmetic  3.57 us (2%)
    ppermute x16, waiting for transfers between devices, along(): return lax.ppermute(v, 'tp', pairs)  44.5 us
    ppermute x16, starting transfers between devices, along(): return lax.ppermute(v, 'tp', pairs)  37.9 us
    all_to_all x1, blocking collectives, body(): recv = lax.all_to_all(send, 'ep', 0, 0, tiled=True)  17 us
    ppermute x6, starting transfers between devices, swapped(): return lax.ppermute(v, 'tp', swap)  16.7 us
    unnamed x30, local copies, waits for them, and re-layouts  9.05 us
    dot_general x9, matrix products, dot(): lax.dot_general(a, b, (((ca,), (cb,)), ((), ())), preferred_element_type=...  6.88 us
    ppermute x6, waiting for transfers between devices, swapped(): return lax.ppermute(v, 'tp', swap)  5.59 us
    pallas_call x1, Pallas kernels, lay_out(): pl.pallas_call(kernel, grid=(steps,), out_shape=[jax.ShapeDtypeStruct((wi...  4.87 us
  transfers between devices with their start and end apart: 24, of which 11 were waited for; matrix products, arithmetic and copies ran while one was open for 1% of the time, Pallas kernels for 6%

commit v1 on v0

--- a/solution.py
+++ b/solution.py
@@ -28,6 +28,87 @@
 
 def smem():
     return pl.BlockSpec(memory_space=pltpu.SMEM)
+
+
+def placed(ids_ref, groups, cap):
+    chosen, n = ids_ref.shape
+    ids = [ids_ref[k : k + 1] for k in range(chosen)]
+    expert = lax.broadcasted_iota(jnp.int32, (groups, n), 0)
+    hot = [(i == expert).astype(F32) for i in ids]
+    t, u = (lax.broadcasted_iota(jnp.int32, (n, n), d) for d in range(2))
+    before = dot(sum(hot).astype(BF), (t < u).astype(BF), 1, 0)
+    slots = [
+        i * cap + jnp.sum(before * h, axis=0, keepdims=True).astype(jnp.int32)
+        for i, h in zip(ids, hot)
+    ]
+    return slots, t == u
+
+
+def column(eye, row):
+    return jnp.sum(jnp.where(eye, row, jnp.zeros_like(row)), axis=1, keepdims=True)
+
+
+def dispatch(tokens, cotangent, ids, weights, groups, cap):
+    n, width = tokens.shape
+    chosen = ids.shape[0]
+    rows = groups * cap
+
+    def kernel(tok, cot, ids_ref, w_ref, out):
+        slots, eye = placed(ids_ref, groups, cap)
+        at = lax.broadcasted_iota(jnp.int32, (rows, n), 0)
+        place = [(at == s).astype(F32).astype(BF) for s in slots]
+        grads = cot[...].astype(F32)
+        sent = dot(sum(place), tok[...], 1, 0)
+        grad = sum(
+            dot(place[k], (column(eye, w_ref[k : k + 1]) * grads).astype(BF), 1, 0)
+            for k in range(chosen)
+        )
+        for g in range(groups):
+            part = slice(g * cap, (g + 1) * cap)
+            out[g] = jnp.concatenate([sent[part], grad[part]], axis=0).astype(BF)
+
+    return pl.pallas_call(
+        kernel,
+        out_shape=jax.ShapeDtypeStruct((groups, 2 * cap, width), BF),
+        in_specs=[vmem()] * 4,
+        out_specs=vmem(),
+        name="dispatch",
+    )(tokens, cotangent, ids, weights)
+
+
+def mix(back, ids, weights, width):
+    groups, both, lanes = back.shape
+    cap = both // 2
+    rows = groups * cap
+    chosen, n = ids.shape
+
+    def kernel(ref, ids_ref, w_ref, mixed, grad, combine):
+        slots, eye = placed(ids_ref, groups, cap)
+        at = lax.broadcasted_iota(jnp.int32, (n, rows), 1)
+        place = [(at == column(eye, s)).astype(F32).astype(BF) for s in slots]
+        blocks = [ref[g].astype(F32) for g in range(groups)]
+        outs = jnp.concatenate([b[:cap] for b in blocks], axis=0).astype(BF)
+        ins = jnp.concatenate([b[cap:] for b in blocks], axis=0).astype(BF)
+        total = jnp.zeros((n, lanes), F32)
+        for k in range(chosen):
+            weight = w_ref[k : k + 1]
+            out = dot(place[k], outs, 1, 0)
+            total += column(eye, weight) * out
+            inner = out[:, width : width + 1] + out[:, width + 1 : width + 2]
+            inner = jnp.sum(jnp.where(eye, inner, 0.0), axis=0, keepdims=True)
+            combine[k : k + 1] = inner / weight
+        mixed[...] = total[:, :width].astype(BF)
+        grad[...] = dot(sum(place), ins, 1, 0)[:, :width].astype(BF)
+
+    return pl.pallas_call(
+        kernel,
+        out_shape=[jax.ShapeDtypeStruct((n, width), BF)] * 2
+        + [jax.ShapeDtypeStruct((chosen, n), F32)],
+        in_specs=[vmem()] * 3,
+        out_specs=[vmem()] * 3,
+        compiler_params=LIMIT,
+        name="mix",
+    )(back, ids, weights)
 
 
 def partials(core, hidden, ggp, gup, wg, wu, wd, chips, width, steps=4):
@@ -82,26 +163,57 @@
     )(core, hidden, ggp, gup, wg, wu, wd)
 
 
-def add_pair(keep, got, extra, steps=2):
+def add_pair(place, keep, got, extra):
     chips, width, lanes = keep.shape
     more = extra.shape[0]
-    each = chips // steps
-
-    def kernel(a, b, e, o):
-        o[:, :width] = (a[...].astype(F32) + b[...].astype(F32)).astype(BF)
-        for i in range(each):
-            o[i, width:] = e[...]
-
-    spec = pl.BlockSpec((each, width, lanes), lambda i: (i, 0, 0))
-    return pl.pallas_call(
-        kernel,
-        grid=(steps,),
-        out_shape=jax.ShapeDtypeStruct((chips, width + more, lanes), BF),
-        in_specs=[spec, spec, pl.BlockSpec((more, lanes), lambda i: (0, 0))],
-        out_specs=pl.BlockSpec((each, width + more, lanes), lambda i: (i, 0, 0)),
+    side = math.isqrt(chips)
+
+    def kernel(at, a, b, e, *outs):
+        first = at[2] == 0
+        for j in range(side):
+            y, x = lax.rem(at[1] + j, side), lax.rem(at[0] + j, side)
+            for i in range(side):
+                chip = jnp.where(first, y * side + i, i * side + x)
+                total = (a[chip].astype(F32) + b[chip].astype(F32)).astype(BF)
+                outs[j][i * width : (i + 1) * width] = total
+            outs[j][side * width :] = e[...]
+
+    return pl.pallas_call(
+        kernel,
+        out_shape=[jax.ShapeDtypeStruct((side * width + more, lanes), BF)] * side,
+        in_specs=[smem(), vmem(), vmem(), vmem()],
+        out_specs=[vmem()] * side,
         compiler_params=LIMIT,
         name="add_pair",
-    )(keep, got, extra)
+    )(place, keep, got, extra)
+
+
+def add_line(place, blocks, width):
+    side = len(blocks)
+    deep, lanes = blocks[0].shape
+    more = deep - side * width
+
+    def kernel(at, *refs):
+        ins, outs = refs[:side], refs[side:]
+        mine = jnp.where(at[2] == 0, at[0], at[1])
+        e = sum(r[side * width :].astype(F32) for r in ins)
+        e = extra_rows(e[0:1] + e[1:2], more).astype(BF)
+        for j in range(side):
+            rows = pl.ds(pl.multiple_of(lax.rem(mine + j, side) * width, 16), width)
+            total = ins[0][rows].astype(F32)
+            for r in ins[1:]:
+                total += r[rows].astype(F32)
+            outs[j][:width] = total.astype(BF)
+            outs[j][width:] = e
+
+    return pl.pallas_call(
+        kernel,
+        out_shape=[jax.ShapeDtypeStruct((width + more, lanes), BF)] * side,
+        in_specs=[smem()] + [vmem()] * side,
+        out_specs=[vmem()] * side,
+        compiler_params=LIMIT,
+        name="add_line",
+    )(place, *blocks)
 
 
 def extra_rows(v, more):
@@ -110,14 +222,14 @@
 
 
 def finish_sum(parts, width, groups):
-    chips, _, lanes = parts.shape
+    n = len(parts)
+    lanes = parts[0].shape[1]
     rows = lanes // 2
     cap = rows // groups
 
-    def kernel(ref, out, turned):
-        total = ref[0].astype(F32)
-        for i in range(1, chips):
-            total += ref[i].astype(F32)
+    def kernel(*refs):
+        out, turned = refs[n:]
+        total = sum(r[...].astype(F32) for r in refs[:n])
         e = total[width : width + 1] + total[width + 1 : width + 2]
         turned[...] = jnp.concatenate([total[:width], extra_rows(e, 128 - width)], axis=0).T
         for g in range(groups):
@@ -129,12 +241,12 @@
     return pl.pallas_call(
         kernel,
         out_shape=jax.ShapeDtypeStruct((groups, 2 * cap, 128), BF),
-        in_specs=[vmem()],
+        in_specs=[vmem()] * n,
         out_specs=vmem(),
         scratch_shapes=[pltpu.VMEM((lanes, 128), F32)],
         compiler_params=LIMIT,
         name="finish_sum",
-    )(parts)
+    )(*parts)
 
 
 def assemble(place, mine, theirs):
@@ -142,40 +254,43 @@
     wide, lanes = mine[0].shape
     width = wide // side
     chips = side * side
+    n = 2 * side
 
     def kernel(at, *refs):
-        full, line = refs[2 * side :]
+        full, line, held, sems = refs[n:]
         x, y, c = at[0], at[1], at[2]
-
-        def chip_of(core, dx, dy):
-            across = lax.rem(x + dx + side, side), lax.rem(y + dy + side, side)
-            down = lax.rem(x + dy + side, side), lax.rem(y + dx + side, side)
-            first = core == 0
-            cx = jnp.where(first, across[0], down[0])
-            cy = jnp.where(first, across[1], down[1])
-            return cy * side + cx
-
+        copies = [pltpu.make_async_copy(refs[p], held.at[p], sems.at[p]) for p in range(n)]
+        for one in copies:
+            one.start()
         for q in range(2):
             core = c if q == 0 else 1 - c
+            first = core == 0
             for j in range(side):
+                copies[q * side + j].wait()
                 for i in range(side):
-                    full[chip_of(core, -i, -j) * 2 + core] = refs[q * side + j][
-                        i * width : (i + 1) * width
-                    ]
-        for q in range(2):
-            core = c if q == 0 else 1 - c
-            for d in range(side):
-                rows = slice((q * side + d) * width, (q * side + d + 1) * width)
-                line[rows] = full[chip_of(c, 0, d) * 2 + core]
+                    x_of = jnp.where(first, x - i, x - j)
+                    y_of = jnp.where(first, y - j, y - i)
+                    chip = lax.rem(y_of + side, side) * side + lax.rem(x_of + side, side)
+                    full[chip * 2 + core] = held[q * side + j, i * width : (i + 1) * width]
+        for d in range(side):
+            back = (side - d) % side
+            line[d * width : (d + 1) * width] = held[back, :width]
+            line[(side + d) * width : (side + d + 1) * width] = held[
+                side, back * width : (back + 1) * width
+            ]
 
     return pl.pallas_call(
         kernel,
         out_shape=[
             jax.ShapeDtypeStruct((2 * chips, width, lanes), BF),
-            jax.ShapeDtypeStruct((2 * side * width, lanes), BF),
+            jax.ShapeDtypeStruct((n * width, lanes), BF),
         ],
-        in_specs=[smem()] + [vmem()] * (2 * side),
+        in_specs=[smem()] + [pl.BlockSpec(memory_space=pltpu.HBM)] * n,
         out_specs=[vmem()] * 2,
+        scratch_shapes=[
+            pltpu.VMEM((n, wide, lanes), BF),
+            pltpu.SemaphoreType.DMA((n,)),
+        ],
         compiler_params=LIMIT,
         name="assemble",
     )(place, *mine, *theirs)
@@ -274,25 +389,8 @@
     def swapped(v):
         return lax.ppermute(v, "tp", swap)
 
-    ids = [expert_ids[:, k] for k in range(chosen)]
-    hot = [
-        (i[:, None] == jnp.arange(groups, dtype=jnp.int32)[None, :]).astype(F32) for i in ids
-    ]
-    both = sum(hot)
-    t = jnp.arange(tok_rows, dtype=jnp.int32)
-    before = jnp.dot((t[:, None] > t[None, :]).astype(F32), both)
-    place = []
-    for k in range(chosen):
-        rank = jnp.sum(before * hot[k], axis=1).astype(jnp.int32)
-        slot = ids[k] * cap + rank
-        place.append((slot[None, :] == jnp.arange(rows, dtype=jnp.int32)[:, None]).astype(BF))
-    cot = cotangent.astype(F32)
-    weight = [combine_weights[:, k][:, None] for k in range(chosen)]
-    send_rows = dot(sum(place), tokens, 1, 0)
-    send_grad = sum(dot(place[k], (weight[k] * cot).astype(BF), 1, 0) for k in range(chosen))
-    send = jnp.concatenate(
-        [send_rows.reshape(groups, cap, width), send_grad.reshape(groups, cap, width)], axis=1
-    ).astype(BF)
+    ids, weights = expert_ids.T, combine_weights.T
+    send = dispatch(tokens, cotangent, ids, weights, groups, cap)
     recv = lax.all_to_all(send, "ep", 0, 0, tiled=True)
     piece = (
         jnp.concatenate(
@@ -331,13 +429,16 @@
     got = swapped(give)
     inner = inner + swapped(inner)
     hi, lo = halves(inner)
-    more = 8
+    more = 16
     extra = jnp.pad(jnp.stack([hi, lo]), ((0, more - 2), (0, rows)))
-    reduced = add_pair(keep, got, extra)
-    same_core = [[2 * i + c for i in range(chips)] for c in range(2)]
-    parts = lax.all_to_all(
-        reduced, "tp", 0, 0, tiled=True, axis_index_groups=same_core
-    )
+    blocks = add_pair(place_now, keep, got, extra)
+
+    def exchanged(blocks, turn):
+        return [blocks[0]] + [along(blocks[d], d, turn) for d in range(1, side)]
+
+    blocks = exchanged(blocks, 1)
+    blocks = add_line(place_now, blocks, width)
+    parts = exchanged(blocks, 0)
     back = finish_sum(parts, width, groups)
 
     grads = weight_grads(line, factors, width)
@@ -359,25 +460,13 @@
     pieces = [pieces[q, d] for q in range(2) for d in range(side)]
 
     back = lax.all_to_all(back, "ep", 0, 0, tiled=True)
-    out_back = back[:, :cap].reshape(rows, -1)
-    in_back = back[:, cap:].reshape(rows, -1)
-    chosen_out = [dot(place[k], out_back, 0, 0) for k in range(chosen)]
-    mixed = sum(weight[k] * chosen_out[k][:, :width] for k in range(chosen)).astype(BF)
-    grad_combine = jnp.concatenate(
-        [
-            (chosen_out[k][:, width : width + 1] + chosen_out[k][:, width + 1 : width + 2])
-            / weight[k]
-            for k in range(chosen)
-        ],
-        axis=1,
-    )
-    grad_tokens = dot(sum(place), in_back[:, :width], 0, 0).astype(BF)
+    mixed, grad_tokens, grad_combine = mix(back, ids, weights, width)
 
     gate_out, up_out, down_out = lay_out(columns, pieces, hid)
     return (
         mixed,
         grad_tokens,
-        grad_combine,
+        grad_combine.T,
         gate_out[None],
         up_out[None],
         down_out.T[None],

time: 169 us -> 137 us (0.81)
  waiting for transfers between devices: 50.1 us -> 39.4 us
  local copies, waits for them, and re-layouts: 11.3 us -> 1.55 us
  starting transfers between devices: 61.7 us -> 52.4 us
  Pallas kernels: 16.3 us -> 21.9 us
  matrix products: 7.02 us -> 3.28 us
  other arithmetic: 3.57 us -> 0.35 us
    ppermute x16 -> x22, waiting for transfers between devices: 44.5 us -> 36 us  [along(): return lax.ppermute(v, 'tp', pairs)]
    unnamed x30 -> x10, local copies, waits for them, and re-layouts: 9.05 us -> 1.22 us
    ppermute x16 -> x22, starting transfers between devices: 37.9 us -> 32.4 us  [along(): return lax.ppermute(v, 'tp', pairs)]
    pallas_call x1 -> x4, Pallas kernels: 0.51 us -> 4.79 us  [the longest x1 1.78 us: dispatch(): pl.pallas_call(kernel, out_shape=jax.ShapeDtypeStruct((groups, 2 * cap, w...]
    all_to_all x1 -> x0, starting transfers between devices: 3.72 us -> none  [body(): lax.all_to_all(reduced, 'tp', 0, 0, tiled=True, axis_index_groups=same_core)]
    dot_general x9 -> x3, matrix products: 6.88 us -> 3.28 us  [dot(): lax.dot_general(a, b, (((ca,), (cb,)), ((), ())), preferred_element_type=...]
    ppermute x6, waiting for transfers between devices: 5.59 us -> 3.4 us  [swapped(): return lax.ppermute(v, 'tp', swap)]
    pallas_call x1, Pallas kernels: 2.03 us -> 3.95 us  [assemble(): pl.pallas_call(kernel, out_shape=[jax.ShapeDtypeStruct((2 * chips, width,...]
  transfers between devices with their start and end apart: 24 -> 29, of which waited for: 11 -> 14; matrix products, arithmetic and copies ran while one was open for 1% -> 0% of each run, Pallas kernels for 6% -> 8%
where the time goes in v1:
time: 137 us
  starting transfers between devices  52.4 us (38%)
  waiting for transfers between devices  39.4 us (29%)
  Pallas kernels  21.9 us (16%)
  blocking collectives  17.2 us (13%)
  matrix products  3.28 us (2%)
  local copies, waits for them, and re-layouts  1.55 us (1%)
    ppermute x22, waiting for transfers between devices, along(): return lax.ppermute(v, 'tp', pairs)  36 us
    ppermute x22, starting transfers between devices, along(): return lax.ppermute(v, 'tp', pairs)  32.4 us
    all_to_all x1, blocking collectives, body(): recv = lax.all_to_all(send, 'ep', 0, 0, tiled=True)  17.2 us
    ppermute x6, starting transfers between devices, swapped(): return lax.ppermute(v, 'tp', swap)  16.7 us
    pallas_call x1, Pallas kernels, lay_out(): pl.pallas_call(kernel, grid=(steps,), out_shape=[jax.ShapeDtypeStruct((wi...  4.41 us
    pallas_call x1, Pallas kernels, weight_grads(): pl.pallas_call(kernel, out_shape=[jax.ShapeDtypeStruct((width, n * 3 * hi...  4.12 us
    pallas_call x1, Pallas kernels, assemble(): pl.pallas_call(kernel, out_shape=[jax.ShapeDtypeStruct((2 * chips, width,...  3.95 us
    pallas_call x1, Pallas kernels, partials(): pl.pallas_call(kernel, grid=(steps,), out_shape=[jax.ShapeDtypeStruct((ch...  3.81 us
  transfers between devices with their start and end apart: 29, of which 14 were waited for; matrix products, arithmetic and copies ran while one was open for 0% of the time, Pallas kernels for 8%

profile of v1, /device:TPU:1, one launch (start us, length us, event | category | flops | bytes accessed | tf_op | source)
XLA Modules:
  0.0 137.0 jit_solution(6717366016841843810)
XLA Ops:
  0.6 1.8 %dispatch.1 = bf16[8,80,96]{2,1,0:T(8,128)(2,1)} custom-call(bf16[96,96]{1,0:T(8,128)(2,1)} %tok.1, bf16[96,96]{1,0:T(8,128)(2,1)} %cot.1, s32[2,96]{1,0:T(2,128)} %bitcast.30, f32[2,96]{1,0:T(2,128)} %bitcast.32), custom_call_target="tpu_custom_call" | custom-call | tf_op jit(solution)/shard_map/dispatch/pallas_call | solution.py:70
  2.4 17.2 %all_to_all.10 = bf16[8,80,96]{2,1,0:T(8,128)(2,1)S(1)} all-to-all(bf16[8,80,96]{2,1,0:T(8,128)(2,1)} %dispatch.1), channel_id=1, replica_groups=mesh['ep'=8,'tp'=32] {'ep'}, dimensions={0} | all-to-all | bytes 245760 | tf_op jit(solution)/shard_map/all_to_all | solution.py:394
  20.0 2.8 %collective-permute-start.2 = (bf16[96,640]{1,0:T(8,128)(2,1)S(1)}, bf16[96,640]{1,0:T(8,128)(2,1)S(1)}, u32[]{:S(2)}, u32[]{:S(2)}) collective-permute-start(bf16[96,640]{1,0:T(8,128)(2,1)S(1)} %maximum_bitcast_fusion), channel_id=1, source_target_pairs={{0,6},{1,25},{2,0},{3,27},{4,2},{5,29},{6,4},{7,31},{8,14},{9,1},{... | collective-permute-start | bytes 368648 | tf_op jit(solution)/shard_map/ppermute | solution.py:387
  23.8 2.1 %collective-permute-done.2 = bf16[96,640]{1,0:T(8,128)(2,1)S(1)} collective-permute-done((bf16[96,640]{1,0:T(8,128)(2,1)S(1)}, bf16[96,640]{1,0:T(8,128)(2,1)S(1)}, u32[]{:S(2)}, u32[]{:S(2)}) %collective-permute-start.2) | collective-permute-done | bytes 122912 | tf_op jit(solution)/shard_map/ppermute | solution.py:387
  25.9 2.2 %collective-permute-done.1 = bf16[96,640]{1,0:T(8,128)(2,1)S(1)} collective-permute-done((bf16[96,640]{1,0:T(8,128)(2,1)S(1)}, bf16[96,640]{1,0:T(8,128)(2,1)S(1)}, u32[]{:S(2)}, u32[]{:S(2)}) %collective-permute-start.1) | collective-permute-done | bytes 122912 | tf_op jit(solution)/shard_map/ppermute | solution.py:387
  30.7 2.7 %collective-permute-start.4 = (bf16[384,640]{1,0:T(8,128)(2,1)S(1)}, bf16[384,640]{1,0:T(8,128)(2,1)S(1)}, u32[]{:S(2)}, u32[]{:S(2)}) collective-permute-start(bf16[384,640]{1,0:T(8,128)(2,1)S(1)} %pad_maximum_fusion.refs_0_), channel_id=1, source_target_pairs={{0,16},{1,5},{2,18},{3,7},{4,20},{5,1},{6,22},{7,3},{8,24},{9,13},... | collective-permute-start | bytes 1474568 | tf_op jit(solution)/shard_map/ppermute | solution.py:387
  34.3 5.9 %collective-permute-start.6 = (bf16[384,640]{1,0:T(8,128)(2,1)S(1)}, bf16[384,640]{1,0:T(8,128)(2,1)S(1)}, u32[]{:S(2)}, u32[]{:S(2)}) collective-permute-start(bf16[384,640]{1,0:T(8,128)(2,1)S(1)} %pad_maximum_fusion.refs_0_), channel_id=1, source_target_pairs={{0,1},{1,0},{2,3},{3,2},{4,5},{5,4},{6,7},{7,6},{8,9},{9,8},{10,11... | collective-permute-start | bytes 1474568 | tf_op jit(solution)/shard_map/ppermute | solution.py:390
  40.2 4.0 %collective-permute-start.7 = (bf16[384,640]{1,0:T(8,128)(2,1)S(1)}, bf16[384,640]{1,0:T(8,128)(2,1)S(1)}, u32[]{:S(2)}, u32[]{:S(2)}) collective-permute-start(bf16[384,640]{1,0:T(8,128)(2,1)S(1)} %collective-permute-done.3.refs_1_), channel_id=1, source_target_pairs={{0,1},{1,0},{2,3},{3,2},{4,5},{5,4},{6,7},{7,6},{8,9},{9,8},{10,11... | collective-permute-start | bytes 1474568 | tf_op jit(solution)/shard_map/ppermute | solution.py:390
  44.9 6.1 %collective-permute-start.8 = (bf16[384,640]{1,0:T(8,128)(2,1)S(1)}, bf16[384,640]{1,0:T(8,128)(2,1)S(1)}, u32[]{:S(2)}, u32[]{:S(2)}) collective-permute-start(bf16[384,640]{1,0:T(8,128)(2,1)S(1)} %collective-permute-done.4.refs_2_), channel_id=1, source_target_pairs={{0,1},{1,0},{2,3},{3,2},{4,5},{5,4},{6,7},{7,6},{8,9},{9,8},{10,11... | collective-permute-start | bytes 1474568 | tf_op jit(solution)/shard_map/ppermute | solution.py:390
  53.3 4.0 %assemble.1 = (bf16[32,96,640]{2,1,0:T(8,128)(2,1)S(1)}, bf16[768,640]{1,0:T(8,128)(2,1)S(1)}) custom-call(s32[3]{0:T(128)S(1)} %pad_add_fusion.at, bf16[384,640]{1,0:T(8,128)(2,1)S(1)} %pad_maximum_fusion.refs_0_, bf16[384,640]{1,0:T(8,128)(2,1)S(1)} %collective-permute-done.3.refs_1_, bf16[384,640]{1,0:T(8,128)(2,1)S(1)} %collective-permute-done.4.refs_2_, ...), custom_call_target="tpu_custom_call" | custom-call | tf_op jit(solution)/shard_map/assemble/pallas_call | solution.py:282
  61.8 3.8 %partials.1 = (bf16[16,96,640]{2,1,0:T(8,128)(2,1)S(1)}, bf16[16,96,640]{2,1,0:T(8,128)(2,1)S(1)}) custom-call(s32[1]{0:T(128)} %bitcast.2.core_ref, bf16[320,256]{1,0:T(8,128)(2,1)S(1)} %get-tuple-element.59.h_ref, bf16[320,256]{1,0:T(8,128)(2,1)S(1)} %get-tuple-element.60.g_ref, bf16[320,256]{1,0:T(8,128)(2,1)S(1)} %get-tuple-element.61.u_ref, ...), custom_call_target="tpu_custom_call" | custom-call | tf_op jit(solution)/shard_map/partials/pallas_call | solution.py:146
  66.9 1.8 %collective-permute-start.19 = (bf16[320,768]{1,0:T(8,128)(2,1)S(1)}, bf16[320,768]{1,0:T(8,128)(2,1)S(1)}, u32[]{:S(2)}, u32[]{:S(2)}) collective-permute-start(bf16[320,768]{1,0:T(8,128)(2,1)S(1)} %pad_maximum_fusion.1.refs_1_), channel_id=1, source_target_pairs={{0,4},{1,17},{2,6},{3,19},{4,0},{5,21},{6,2},{7,23},{8,12},{9,25},... | collective-permute-start | bytes 1474568 | tf_op jit(solution)/shard_map/ppermute | solution.py:387
  72.6 1.8 %collective-permute-start.13 = (bf16[400,640]{1,0:T(8,128)(2,1)S(1)}, bf16[400,640]{1,0:T(8,128)(2,1)S(1)}, u32[]{:S(2)}, u32[]{:S(2)}) collective-permute-start(bf16[400,640]{1,0:T(8,128)(2,1)S(1)} %get-tuple-element.37), channel_id=1, source_target_pairs={{0,16},{1,5},{2,18},{3,7},{4,20},{5,1},{6,22},{7,3},{8,24},{9,13},... | collective-permute-start | bytes 1536008 | tf_op jit(solution)/shard_map/ppermute | solution.py:387
  74.4 2.3 %collective-permute-done.18.refs_2_ = bf16[320,768]{1,0:T(8,128)(2,1)S(1)} collective-permute-done((bf16[320,768]{1,0:T(8,128)(2,1)S(1)}, bf16[320,768]{1,0:T(8,128)(2,1)S(1)}, u32[]{:S(2)}, u32[]{:S(2)}) %collective-permute-start.18) | collective-permute-done | bytes 491552 | tf_op jit(solution)/shard_map/ppermute | solution.py:387
  77.5 7.0 %collective-permute-done.19.refs_3_ = bf16[320,768]{1,0:T(8,128)(2,1)S(1)} collective-permute-done((bf16[320,768]{1,0:T(8,128)(2,1)S(1)}, bf16[320,768]{1,0:T(8,128)(2,1)S(1)}, u32[]{:S(2)}, u32[]{:S(2)}) %collective-permute-start.19) | collective-permute-done | bytes 491552 | tf_op jit(solution)/shard_map/ppermute | solution.py:387
  84.8 4.1 %weight_grads.1 = (bf16[96,3072]{1,0:T(8,128)(2,1)S(1)}, bf16[96,3072]{1,0:T(8,128)(2,1)S(1)}, bf16[96,3072]{1,0:T(8,128)(2,1)S(1)}, bf16[96,3072]{1,0:T(8,128)(...) custom-call(bf16[768,640]{1,0:T(8,128)(2,1)S(1)} %get-tuple-element., ...), custom_call_target="tpu_custom_call" | custom-call | tf_op jit(solution)/shard_map/weight_grads/pallas_call | solution.py:325
  90.2 1.9 %collective-permute-done.12.refs_1_ = bf16[400,640]{1,0:T(8,128)(2,1)S(1)} collective-permute-done((bf16[400,640]{1,0:T(8,128)(2,1)S(1)}, bf16[400,640]{1,0:T(8,128)(2,1)S(1)}, u32[]{:S(2)}, u32[]{:S(2)}) %collective-permute-start.12) | collective-permute-done | bytes 512032 | tf_op jit(solution)/shard_map/ppermute | solution.py:387
  94.5 2.0 %collective-permute-start.16 = (bf16[112,640]{1,0:T(8,128)(2,1)S(1)}, bf16[112,640]{1,0:T(8,128)(2,1)S(1)}, u32[]{:S(2)}, u32[]{:S(2)}) collective-permute-start(bf16[112,640]{1,0:T(8,128)(2,1)S(1)} %get-tuple-element.41), channel_id=1, source_target_pairs={{0,4},{1,17},{2,6},{3,19},{4,0},{5,21},{6,2},{7,23},{8,12},{9,25},... | collective-permute-start | bytes 430088 | tf_op jit(solution)/shard_map/ppermute | solution.py:387
  97.8 8.7 %collective-permute-done.21.refs_1_ = bf16[96,3072]{1,0:T(8,128)(2,1)S(1)} collective-permute-done((bf16[96,3072]{1,0:T(8,128)(2,1)S(1)}, bf16[96,3072]{1,0:T(8,128)(2,1)S(1)}, u32[]{:S(2)}, u32[]{:S(2)}) %collective-permute-start.21) | collective-permute-done | bytes 589856 | tf_op jit(solution)/shard_map/ppermute | solution.py:387
  106.5 7.4 %collective-permute-start.24 = (bf16[96,3072]{1,0:T(8,128)(2,1)}, bf16[96,3072]{1,0:T(8,128)(2,1)S(1)}, u32[]{:S(2)}, u32[]{:S(2)}) collective-permute-start(bf16[96,3072]{1,0:T(8,128)(2,1)} %get-tuple-element.51), channel_id=1, source_target_pairs={{0,1},{1,0},{2,3},{3,2},{4,5},{5,4},{6,7},{7,6},{8,9},{9,8},{10,11... | collective-permute-start | bytes 1769480 | tf_op jit(solution)/shard_map/ppermute | solution.py:387
  115.3 2.9 %collective-permute-start.27 = (bf16[96,3072]{1,0:T(8,128)(2,1)}, bf16[96,3072]{1,0:T(8,128)(2,1)}, u32[]{:S(2)}, u32[]{:S(2)}) collective-permute-start(bf16[96,3072]{1,0:T(8,128)(2,1)} %get-tuple-element.54), channel_id=1, source_target_pairs={{0,25},{1,6},{2,27},{3,0},{4,29},{5,2},{6,31},{7,4},{8,1},{9,14},{... | collective-permute-start | bytes 1769480 | tf_op jit(solution)/shard_map/ppermute | solution.py:387
  119.0 3.4 %all-to-all-start.1 = ((bf16[8,80,128]{2,1,0:T(8,128)(2,1)}), bf16[8,80,128]{2,1,0:T(8,128)(2,1)S(1)}, u32[]{:S(2)}, u32[]{:S(2)}) async-start(bf16[8,80,128]{2,1,0:T(8,128)(2,1)} %finish_sum.1), calls=%async_computation.1 | async-start | bytes 327680 | tf_op jit(solution)/shard_map/all_to_all | solution.py:462
  122.6 8.8 %collective-permute-done.25.refs_5_ = bf16[96,3072]{1,0:T(8,128)(2,1)} collective-permute-done((bf16[96,3072]{1,0:T(8,128)(2,1)}, bf16[96,3072]{1,0:T(8,128)(2,1)}, u32[]{:S(2)}, u32[]{:S(2)}) %collective-permute-start.25) | collective-permute-done | bytes 589856 | tf_op jit(solution)/shard_map/ppermute | solution.py:387
  131.4 4.4 %lay_out.1 = (bf16[96,8192]{1,0:T(8,128)(2,1)}, bf16[96,8192]{1,0:T(8,128)(2,1)}, bf16[96,8192]{1,0:T(8,128)(2,1)}) custom-call(s32[32]{0:T(128)S(1)} %concatenate.14.cols, bf16[96,3072]{1,0:T(8,128)(2,1)S(1)} %get-tuple-element.47.refs_0_, bf16[96,3072]{1,0:T(8,128)(2,1)S(1)} %collective-permute-done.21.refs_1_, ...), custom_call_target="tpu_custom_call" | custom-call | tf_op jit(solution)/shard_map/lay_out/pallas_call | solution.py:352
  (73 shorter events, 27.1 us)
Async XLA Ops:
  23.2 6.2 %collective-permute-start = (bf16[96,640]{1,0:T(8,128)(2,1)S(1)}, bf16[96,640]{1,0:T(8,128)(2,1)S(1)}, u32[]{:S(2)}, u32[]{:S(2)}) collective-permute-start(bf16[96,640]{1,0:T(8,128)(2,1)S(1)} %maximum_bitcast_fusion), channel_id=1, source_target_pairs={{0,2},{1,9},{2,4},{3,11},{4,6},{5,13},{6,0},{7,15},{8,10},{9,17},{... | collective-permute-start | bytes 368648 | tf_op jit(solution)/shard_map/ppermute | solution.py:387
  29.4 10.9 %collective-permute-start.3 = (bf16[384,640]{1,0:T(8,128)(2,1)S(1)}, bf16[384,640]{1,0:T(8,128)(2,1)S(1)}, u32[]{:S(2)}, u32[]{:S(2)}) collective-permute-start(bf16[384,640]{1,0:T(8,128)(2,1)S(1)} %pad_maximum_fusion.refs_0_), channel_id=1, source_target_pairs={{0,8},{1,3},{2,10},{3,5},{4,12},{5,7},{6,14},{7,1},{8,16},{9,11},{... | collective-permute-start | bytes 1474568 | tf_op jit(solution)/shard_map/ppermute | solution.py:387
  30.7 14.2 %collective-permute-start.4 = (bf16[384,640]{1,0:T(8,128)(2,1)S(1)}, bf16[384,640]{1,0:T(8,128)(2,1)S(1)}, u32[]{:S(2)}, u32[]{:S(2)}) collective-permute-start(bf16[384,640]{1,0:T(8,128)(2,1)S(1)} %pad_maximum_fusion.refs_0_), channel_id=1, source_target_pairs={{0,16},{1,5},{2,18},{3,7},{4,20},{5,1},{6,22},{7,3},{8,24},{9,13},... | collective-permute-start | bytes 1474568 | tf_op jit(solution)/shard_map/ppermute | solution.py:387
  33.4 17.6 %collective-permute-start.5 = (bf16[384,640]{1,0:T(8,128)(2,1)S(1)}, bf16[384,640]{1,0:T(8,128)(2,1)S(1)}, u32[]{:S(2)}, u32[]{:S(2)}) collective-permute-start(bf16[384,640]{1,0:T(8,128)(2,1)S(1)} %pad_maximum_fusion.refs_0_), channel_id=1, source_target_pairs={{0,24},{1,7},{2,26},{3,1},{4,28},{5,3},{6,30},{7,5},{8,0},{9,15},{... | collective-permute-start | bytes 1474568 | tf_op jit(solution)/shard_map/ppermute | solution.py:387
  34.3 16.8 %collective-permute-start.6 = (bf16[384,640]{1,0:T(8,128)(2,1)S(1)}, bf16[384,640]{1,0:T(8,128)(2,1)S(1)}, u32[]{:S(2)}, u32[]{:S(2)}) collective-permute-start(bf16[384,640]{1,0:T(8,128)(2,1)S(1)} %pad_maximum_fusion.refs_0_), channel_id=1, source_target_pairs={{0,1},{1,0},{2,3},{3,2},{4,5},{5,4},{6,7},{7,6},{8,9},{9,8},{10,11... | collective-permute-start | bytes 1474568 | tf_op jit(solution)/shard_map/ppermute | solution.py:390
  40.2 10.8 %collective-permute-start.7 = (bf16[384,640]{1,0:T(8,128)(2,1)S(1)}, bf16[384,640]{1,0:T(8,128)(2,1)S(1)}, u32[]{:S(2)}, u32[]{:S(2)}) collective-permute-start(bf16[384,640]{1,0:T(8,128)(2,1)S(1)} %collective-permute-done.3.refs_1_), channel_id=1, source_target_pairs={{0,1},{1,0},{2,3},{3,2},{4,5},{5,4},{6,7},{7,6},{8,9},{9,8},{10,11... | collective-permute-start | bytes 1474568 | tf_op jit(solution)/shard_map/ppermute | solution.py:390
  44.9 7.6 %collective-permute-start.8 = (bf16[384,640]{1,0:T(8,128)(2,1)S(1)}, bf16[384,640]{1,0:T(8,128)(2,1)S(1)}, u32[]{:S(2)}, u32[]{:S(2)}) collective-permute-start(bf16[384,640]{1,0:T(8,128)(2,1)S(1)} %collective-permute-done.4.refs_2_), channel_id=1, source_target_pairs={{0,1},{1,0},{2,3},{3,2},{4,5},{5,4},{6,7},{7,6},{8,9},{9,8},{10,11... | collective-permute-start | bytes 1474568 | tf_op jit(solution)/shard_map/ppermute | solution.py:390
  66.3 10.5 %collective-permute-start.18 = (bf16[320,768]{1,0:T(8,128)(2,1)S(1)}, bf16[320,768]{1,0:T(8,128)(2,1)S(1)}, u32[]{:S(2)}, u32[]{:S(2)}) collective-permute-start(bf16[320,768]{1,0:T(8,128)(2,1)S(1)} %pad_maximum_fusion.1.refs_1_), channel_id=1, source_target_pairs={{0,2},{1,9},{2,4},{3,11},{4,6},{5,13},{6,0},{7,15},{8,10},{9,17},{... | collective-permute-start | bytes 1474568 | tf_op jit(solution)/shard_map/ppermute | solution.py:387
  66.9 17.7 %collective-permute-start.19 = (bf16[320,768]{1,0:T(8,128)(2,1)S(1)}, bf16[320,768]{1,0:T(8,128)(2,1)S(1)}, u32[]{:S(2)}, u32[]{:S(2)}) collective-permute-start(bf16[320,768]{1,0:T(8,128)(2,1)S(1)} %pad_maximum_fusion.1.refs_1_), channel_id=1, source_target_pairs={{0,4},{1,17},{2,6},{3,19},{4,0},{5,21},{6,2},{7,23},{8,12},{9,25},... | collective-permute-start | bytes 1474568 | tf_op jit(solution)/shard_map/ppermute | solution.py:387
  68.7 16.1 %collective-permute-start.20 = (bf16[320,768]{1,0:T(8,128)(2,1)S(1)}, bf16[320,768]{1,0:T(8,128)(2,1)S(1)}, u32[]{:S(2)}, u32[]{:S(2)}) collective-permute-start(bf16[320,768]{1,0:T(8,128)(2,1)S(1)} %pad_maximum_fusion.1.refs_1_), channel_id=1, source_target_pairs={{0,6},{1,25},{2,0},{3,27},{4,2},{5,29},{6,4},{7,31},{8,14},{9,1},{... | collective-permute-start | bytes 1474568 | tf_op jit(solution)/shard_map/ppermute | solution.py:387
  72.5 19.5 %collective-permute-start.12 = (bf16[400,640]{1,0:T(8,128)(2,1)S(1)}, bf16[400,640]{1,0:T(8,128)(2,1)S(1)}, u32[]{:S(2)}, u32[]{:S(2)}) collective-permute-start(bf16[400,640]{1,0:T(8,128)(2,1)S(1)} %get-tuple-element.36), channel_id=1, source_target_pairs={{0,8},{1,3},{2,10},{3,5},{4,12},{5,7},{6,14},{7,1},{8,16},{9,11},{... | collective-permute-start | bytes 1536008 | tf_op jit(solution)/shard_map/ppermute | solution.py:387
  72.6 19.5 %collective-permute-start.13 = (bf16[400,640]{1,0:T(8,128)(2,1)S(1)}, bf16[400,640]{1,0:T(8,128)(2,1)S(1)}, u32[]{:S(2)}, u32[]{:S(2)}) collective-permute-start(bf16[400,640]{1,0:T(8,128)(2,1)S(1)} %get-tuple-element.37), channel_id=1, source_target_pairs={{0,16},{1,5},{2,18},{3,7},{4,20},{5,1},{6,22},{7,3},{8,24},{9,13},... | collective-permute-start | bytes 1536008 | tf_op jit(solution)/shard_map/ppermute | solution.py:387
  76.7 16.2 %collective-permute-start.14 = (bf16[400,640]{1,0:T(8,128)(2,1)S(1)}, bf16[400,640]{1,0:T(8,128)(2,1)S(1)}, u32[]{:S(2)}, u32[]{:S(2)}) collective-permute-start(bf16[400,640]{1,0:T(8,128)(2,1)S(1)} %get-tuple-element.38), channel_id=1, source_target_pairs={{0,24},{1,7},{2,26},{3,1},{4,28},{5,3},{6,30},{7,5},{8,0},{9,15},{... | collective-permute-start | bytes 1536008 | tf_op jit(solution)/shard_map/ppermute | solution.py:387
  89.0 17.6 %collective-permute-start.21 = (bf16[96,3072]{1,0:T(8,128)(2,1)S(1)}, bf16[96,3072]{1,0:T(8,128)(2,1)S(1)}, u32[]{:S(2)}, u32[]{:S(2)}) collective-permute-start(bf16[96,3072]{1,0:T(8,128)(2,1)S(1)} %get-tuple-element.48), channel_id=1, source_target_pairs={{0,8},{1,3},{2,10},{3,5},{4,12},{5,7},{6,14},{7,1},{8,16},{9,11},{... | collective-permute-start | bytes 1769480 | tf_op jit(solution)/shard_map/ppermute | solution.py:387
  89.3 17.2 %collective-permute-start.22 = (bf16[96,3072]{1,0:T(8,128)(2,1)S(1)}, bf16[96,3072]{1,0:T(8,128)(2,1)S(1)}, u32[]{:S(2)}, u32[]{:S(2)}) collective-permute-start(bf16[96,3072]{1,0:T(8,128)(2,1)S(1)} %get-tuple-element.49), channel_id=1, source_target_pairs={{0,16},{1,5},{2,18},{3,7},{4,20},{5,1},{6,22},{7,3},{8,24},{9,13},... | collective-permute-start | bytes 1769480 | tf_op jit(solution)/shard_map/ppermute | solution.py:387
  93.8 20.1 %collective-permute-start.15 = (bf16[112,640]{1,0:T(8,128)(2,1)S(1)}, bf16[112,640]{1,0:T(8,128)(2,1)S(1)}, u32[]{:S(2)}, u32[]{:S(2)}) collective-permute-start(bf16[112,640]{1,0:T(8,128)(2,1)S(1)} %get-tuple-element.40), channel_id=1, source_target_pairs={{0,2},{1,9},{2,4},{3,11},{4,6},{5,13},{6,0},{7,15},{8,10},{9,17},{... | collective-permute-start | bytes 430088 | tf_op jit(solution)/shard_map/ppermute | solution.py:387
  94.5 19.3 %collective-permute-start.16 = (bf16[112,640]{1,0:T(8,128)(2,1)S(1)}, bf16[112,640]{1,0:T(8,128)(2,1)S(1)}, u32[]{:S(2)}, u32[]{:S(2)}) collective-permute-start(bf16[112,640]{1,0:T(8,128)(2,1)S(1)} %get-tuple-element.41), channel_id=1, source_target_pairs={{0,4},{1,17},{2,6},{3,19},{4,0},{5,21},{6,2},{7,23},{8,12},{9,25},... | collective-permute-start | bytes 430088 | tf_op jit(solution)/shard_map/ppermute | solution.py:387
  96.5 18.8 %collective-permute-start.17 = (bf16[112,640]{1,0:T(8,128)(2,1)S(1)}, bf16[112,640]{1,0:T(8,128)(2,1)S(1)}, u32[]{:S(2)}, u32[]{:S(2)}) collective-permute-start(bf16[112,640]{1,0:T(8,128)(2,1)S(1)} %get-tuple-element.42), channel_id=1, source_target_pairs={{0,6},{1,25},{2,0},{3,27},{4,2},{5,29},{6,4},{7,31},{8,14},{9,1},{... | collective-permute-start | bytes 430088 | tf_op jit(solution)/shard_map/ppermute | solution.py:387
  106.5 16.0 %collective-permute-start.23 = (bf16[96,3072]{1,0:T(8,128)(2,1)}, bf16[96,3072]{1,0:T(8,128)(2,1)S(1)}, u32[]{:S(2)}, u32[]{:S(2)}) collective-permute-start(bf16[96,3072]{1,0:T(8,128)(2,1)} %get-tuple-element.50), channel_id=1, source_target_pairs={{0,24},{1,7},{2,26},{3,1},{4,28},{5,3},{6,30},{7,5},{8,0},{9,15},{... | collective-permute-start | bytes 1769480 | tf_op jit(solution)/shard_map/ppermute | solution.py:387
  106.5 16.0 %collective-permute-start.24 = (bf16[96,3072]{1,0:T(8,128)(2,1)}, bf16[96,3072]{1,0:T(8,128)(2,1)S(1)}, u32[]{:S(2)}, u32[]{:S(2)}) collective-permute-start(bf16[96,3072]{1,0:T(8,128)(2,1)} %get-tuple-element.51), channel_id=1, source_target_pairs={{0,1},{1,0},{2,3},{3,2},{4,5},{5,4},{6,7},{7,6},{8,9},{9,8},{10,11... | collective-permute-start | bytes 1769480 | tf_op jit(solution)/shard_map/ppermute | solution.py:387
  113.9 17.5 %collective-permute-start.25 = (bf16[96,3072]{1,0:T(8,128)(2,1)}, bf16[96,3072]{1,0:T(8,128)(2,1)}, u32[]{:S(2)}, u32[]{:S(2)}) collective-permute-start(bf16[96,3072]{1,0:T(8,128)(2,1)} %get-tuple-element.52), channel_id=1, source_target_pairs={{0,9},{1,2},{2,11},{3,4},{4,13},{5,6},{6,15},{7,0},{8,17},{9,10},{... | collective-permute-start | bytes 1769480 | tf_op jit(solution)/shard_map/ppermute | solution.py:387
  113.9 17.4 %collective-permute-start.26 = (bf16[96,3072]{1,0:T(8,128)(2,1)}, bf16[96,3072]{1,0:T(8,128)(2,1)}, u32[]{:S(2)}, u32[]{:S(2)}) collective-permute-start(bf16[96,3072]{1,0:T(8,128)(2,1)} %get-tuple-element.53), channel_id=1, source_target_pairs={{0,17},{1,4},{2,19},{3,6},{4,21},{5,0},{6,23},{7,2},{8,25},{9,12},... | collective-permute-start | bytes 1769480 | tf_op jit(solution)/shard_map/ppermute | solution.py:387
  115.3 16.1 %collective-permute-start.27 = (bf16[96,3072]{1,0:T(8,128)(2,1)}, bf16[96,3072]{1,0:T(8,128)(2,1)}, u32[]{:S(2)}, u32[]{:S(2)}) collective-permute-start(bf16[96,3072]{1,0:T(8,128)(2,1)} %get-tuple-element.54), channel_id=1, source_target_pairs={{0,25},{1,6},{2,27},{3,0},{4,29},{5,2},{6,31},{7,4},{8,1},{9,14},{... | collective-permute-start | bytes 1769480 | tf_op jit(solution)/shard_map/ppermute | solution.py:387
  119.0 16.8 %all-to-all-start.1 = ((bf16[8,80,128]{2,1,0:T(8,128)(2,1)}), bf16[8,80,128]{2,1,0:T(8,128)(2,1)S(1)}, u32[]{:S(2)}, u32[]{:S(2)}) async-start(bf16[8,80,128]{2,1,0:T(8,128)(2,1)} %finish_sum.1), calls=%async_computation.1 | async-start | bytes 327680 | tf_op jit(solution)/shard_map/all_to_all | solution.py:462
  (10 other events, 38.6 us)
